TPU v7x, 32 devices: a whole 2x2x4 slice. The times are simulated.
32 devices in a mesh: stn: 4 (over z), chan: 4 (over y, core), tile: 2 (over x).
Axes of the slice: x: 2, y: 2, z: 4, core: 2. Of those that a mesh axis runs over, the one named last changes fastest.
Arguments:
- model_image: bfloat16 [8, 64, 2048], P('tile', 'stn'), may hold values from -0.005859375 to 0.005859375
- station_beams: float32 [2, 64, 1024], replicated, may hold values from -6 to 6
- subgrid_offsets: int32 [4, 128, 2], P('chan'), may hold values from -4096 to 4064
- subgrid_stations: int32 [128, 2], P(('stn', 'tile')), may hold values from 0 to 63, as said below
- visibility_uv: float32 [2, 128, 512], P(None, ('stn', 'tile'), 'chan'), may hold values from 2 to 30
- observed: float32 [2, 32, 4, 512], P(None, ('stn', 'tile'), 'chan'), may hold values from -3 to 3
- live_counts: int32 [32, 4], P(('stn', 'tile'), 'chan'), may hold values from 1 to 8
Outputs:
- residual: float32 [2, 32, 4, 512], P(None, ('stn', 'tile'), 'chan')
Inputs may be any that keep to these rules, and one draw needn't show every extreme that they name: `subgrid_stations`: each row names two different stations. `live_counts`: rows with a time step at or beyond the count carry no data.
All inputs are finite; a program needn't handle non-finite values.
Results may differ from a plain program's by a relative error of at most 0.00071.
Values may be sent and summed in bfloat16 or wider, within the bound.
A program may use at most 64 MiB of HBM per device.

v0:
```python
import math

import jax
import jax.numpy as jnp
from jax import lax
from jax.sharding import PartitionSpec as P

SG = 32
NG = 8192
TIMES = 8
TILE_DEV = 4
TL = 64
SUB_TILE = 16


two_pi = 6.283185307179586


def phase_pair(products, modulus):
    angle_turns = jnp.mod(products, modulus).astype(jnp.float32) * (two_pi / modulus)
    return (jnp.cos(angle_turns), -jnp.sin(angle_turns))


def narrow_mix(pattern, left, right):
    return jnp.einsum(pattern, left, right, preferred_element_type=jnp.float32)


def exact_mix(pattern, left, right):
    return jnp.einsum(pattern, left, right, precision=lax.Precision.HIGHEST)


def tile_cuts(strip_rows, row_ids, offset_block, strip_half):
    block_size = offset_block.shape[0]
    columns = strip_rows.shape[1]
    pixel_idx = jnp.arange(SG, dtype=jnp.int32)
    col_pos = jnp.arange(columns, dtype=jnp.int32) - columns // 2
    v_index = offset_block[:, 1][:, None] + pixel_idx[None, :]
    ev_real, ev_imag = phase_pair(col_pos[:, None, None] * v_index[None, :, :], NG)
    phase_table = (
        jnp.stack([ev_real, ev_imag], axis=1)
        .reshape(columns, 2 * block_size * SG)
        .astype(jnp.bfloat16)
    )
    partial_q = jnp.dot(strip_rows, phase_table, preferred_element_type=jnp.float32).astype(
        jnp.bfloat16
    )
    partial_q = partial_q.reshape(strip_rows.shape[0], 2, block_size, SG)
    q_real = partial_q[:, 0]
    q_imag = partial_q[:, 1]
    u_index = offset_block[:, 0][:, None] + pixel_idx[None, :]
    row_pos = row_ids - strip_half
    eu_real, eu_imag = phase_pair(u_index[:, :, None] * row_pos[None, None, :], NG)
    eu_real = eu_real.astype(jnp.bfloat16)
    eu_imag = eu_imag.astype(jnp.bfloat16)
    cut_real = narrow_mix("jal,ljb->jab", eu_real, q_real) - narrow_mix(
        "jal,ljb->jab", eu_imag, q_imag
    )
    cut_imag = narrow_mix("jal,ljb->jab", eu_real, q_imag) + narrow_mix(
        "jal,ljb->jab", eu_imag, q_real
    )
    return jnp.stack([cut_real, cut_imag], axis=1).reshape(block_size, 2 * SG * SG)


def cuts_blocked(strip_rows, row_ids, offsets, strip_half):
    how_many = offsets.shape[0]
    block_size = math.gcd(how_many, 32)
    grouped = offsets.reshape(how_many // block_size, block_size, 2)
    stacked = lax.map(
        lambda offset_block: tile_cuts(strip_rows, row_ids, offset_block, strip_half), grouped
    )
    return stacked.reshape(how_many, 2 * SG * SG)


def predict(cut_rows, pair_ids, station_beams, uv_block):
    how_many = cut_rows.shape[0]
    cut_grid = cut_rows.reshape(how_many, 2, SG, SG)
    pixel_idx = jnp.arange(SG, dtype=jnp.int32)
    w_real, w_neg = phase_pair(pixel_idx[:, None] * pixel_idx[None, :], SG)
    w_imag = -w_neg
    c_real = cut_grid[:, 0]
    c_imag = cut_grid[:, 1]
    half_real = exact_mix("xa,jab->jxb", w_real, c_real) - exact_mix("xa,jab->jxb", w_imag, c_imag)
    half_imag = exact_mix("xa,jab->jxb", w_real, c_imag) + exact_mix("xa,jab->jxb", w_imag, c_real)
    sub_real = (
        exact_mix("jxb,yb->jxy", half_real, w_real) - exact_mix("jxb,yb->jxy", half_imag, w_imag)
    ) / (SG * SG)
    sub_imag = (
        exact_mix("jxb,yb->jxy", half_real, w_imag) + exact_mix("jxb,yb->jxy", half_imag, w_real)
    ) / (SG * SG)
    pixel_pos = pixel_idx.astype(jnp.float32)
    taper_line = 1.0 - ((2.0 * pixel_pos - (SG - 1)) / SG) ** 2
    taper_grid = (taper_line[:, None] * taper_line[None, :]).reshape(SG * SG)
    beam_first = station_beams[:, pair_ids[:, 0]]
    beam_second = station_beams[:, pair_ids[:, 1]]
    gain_real = (beam_first[0] * beam_second[0] + beam_first[1] * beam_second[1]) * taper_grid
    gain_imag = (beam_first[1] * beam_second[0] - beam_first[0] * beam_second[1]) * taper_grid
    flat_real = sub_real.reshape(how_many, SG * SG)
    flat_imag = sub_imag.reshape(how_many, SG * SG)
    weighted_real = (flat_real * gain_real - flat_imag * gain_imag).reshape(how_many, SG, SG)
    weighted_imag = (flat_real * gain_imag + flat_imag * gain_real).reshape(how_many, SG, SG)
    u_angle = uv_block[0][:, :, None] * pixel_pos[None, None, :] * (two_pi / SG)
    v_angle = uv_block[1][:, :, None] * pixel_pos[None, None, :] * (two_pi / SG)
    eu_real = jnp.cos(u_angle)
    eu_imag = -jnp.sin(u_angle)
    ev_real = jnp.cos(v_angle)
    ev_imag = -jnp.sin(v_angle)
    inner_real = exact_mix("jxy,jky->jxk", weighted_real, ev_real) - exact_mix(
        "jxy,jky->jxk", weighted_imag, ev_imag
    )
    inner_imag = exact_mix("jxy,jky->jxk", weighted_real, ev_imag) + exact_mix(
        "jxy,jky->jxk", weighted_imag, ev_real
    )
    vis_real = exact_mix("jkx,jxk->jk", eu_real, inner_real) - exact_mix(
        "jkx,jxk->jk", eu_imag, inner_imag
    )
    vis_imag = exact_mix("jkx,jxk->jk", eu_real, inner_imag) + exact_mix(
        "jkx,jxk->jk", eu_imag, inner_real
    )
    return jnp.stack([vis_real, vis_imag], axis=0)


def on_device(
    model_image,
    station_beams,
    subgrid_offsets,
    subgrid_stations,
    visibility_uv,
    observed,
    live_counts,
):
    tile_count = lax.axis_size("tile")
    columns = model_image.shape[2]
    strip_half = TILE_DEV * tile_count * TL // 2
    group_offsets = subgrid_offsets[0]
    stn_index = lax.axis_index("stn")
    tile_first = lax.axis_index("tile") * TILE_DEV
    tile_ids = jnp.arange(TILE_DEV, dtype=jnp.int32)
    group_size = SUB_TILE * tile_count
    station_offsets = lax.dynamic_slice_in_dim(group_offsets, stn_index * group_size, group_size, 0)
    shard_piece = lax.all_gather(model_image, "stn", axis=1, tiled=True)
    piece_rows = shard_piece.shape[1]
    piece_ids = (
        (tile_first + tile_ids)[:, None] * TL + jnp.arange(piece_rows, dtype=jnp.int32)[None, :]
    ).reshape(-1)
    piece_strip = shard_piece.reshape(TILE_DEV * piece_rows, columns)
    group_cuts = cuts_blocked(piece_strip, piece_ids, station_offsets, strip_half)
    own_cuts = lax.psum_scatter(group_cuts, "tile", scatter_dimension=0, tiled=True)
    predicted = predict(own_cuts, subgrid_stations, station_beams, visibility_uv)
    chan_count = lax.axis_size("chan")
    outgoing = predicted.reshape(2, SUB_TILE // chan_count, chan_count, predicted.shape[2])
    regrouped = lax.all_to_all(outgoing, "chan", split_axis=2, concat_axis=3, tiled=True)
    total_rows = regrouped.shape[3]
    time_step = jnp.mod(jnp.arange(total_rows, dtype=jnp.int32), TIMES)
    live_mask = time_step[None, None, :] < live_counts[:, :, None]
    return jnp.where(live_mask[None], observed - regrouped, 0.0)


def solution(mesh):
    return jax.shard_map(
        on_device,
        mesh=mesh,
        in_specs=(
            P("tile", "stn", None),
            P(),
            P("chan", None, None),
            P(("stn", "tile"), None),
            P(None, ("stn", "tile"), "chan"),
            P(None, ("stn", "tile"), "chan", None),
            P(("stn", "tile"), "chan"),
        ),
        out_specs=P(None, ("stn", "tile"), "chan", None),
        check_vma=False,
    )
```

profile of v0, /device:TPU:0, one launch (start us, length us, event | category | flops | bytes accessed | tf_op | source)
XLA Modules:
  0.0 118.8 jit_solution(3581766435553474679)
XLA Ops:
  6.5 0.0 copy-start
  6.5 0.0 all-gather.2.cloned.1.call-start
  6.5 0.7 all-gather.2.cloned.1.call-update
  7.3 0.0 reduce-scatter.2.cloned.1.call-start
  7.3 0.8 dynamic-slice_bitcast_fusion
  8.1 0.1 iota_add_fusion
  8.2 0.1 iota_add_fusion.1
  8.2 0.1 add_add_fusion
  8.3 0.8 fusion.66
  9.1 0.0 copy-done
  9.1 0.7 gather_fusion
  9.9 0.7 gather_fusion.1
  10.6 0.1 sub.67
  10.7 0.1 add.237
  10.8 0.1 sub.77
  11.0 35.5 %cosine_convert_fusion = (bf16[2048,1,32,32]{0,3,2,1:T(8,128)(2,1)S(1)}, bf16[2048,1,32,32]{0,3,2,1:T(8,128)(2,1)}) fusion(s32[32,32]{1,0:T(8,128)S(1)} %iota_add_fusion, s32[2048]{0:T(1024)S(1)} %iota_add_fusion.2), kind=kLoop, calls=%fused_computation.12 | loop fusion | flops 35651584 | bytes 8400896 | tf_op jit(solution)/shard_map/convert
  46.4 6.2 %pad_maximum_fusion = bf16[2048,2,32,32]{0,3,2,1:T(8,128)(2,1)} fusion(bf16[2048,1,32,32]{0,3,2,1:T(8,128)(2,1)} %get-tuple-element.31, bf16[2048,1,32,32]{0,3,2,1:T(8,128)(2,1)S(1)} %get-tuple-element.30), kind=kLoop, calls=%fused_computation.10 | loop fusion | flops 4194304 | bytes 16777216 | tf_op jit(solution)/shard_map/while/body/eval_jaxpr/stack | solution.py:40
  52.6 0.0 all-gather.2.cloned.1.call-done
  52.6 6.0 %convolution_convert_fusion = bf16[2048,256]{1,0:T(8,128)(2,1)S(1)} fusion(bf16[2048,2048]{0,1:T(8,128)(2,1)} %bitcast.90, bf16[256,2048]{1,0:T(8,128)(2,1)} %bitcast.96), kind=kOutput, calls=%fused_computation.13 | convolution fusion | flops 2148007936 | bytes 10485760 | tf_op jit(solution)/shard_map/while/body/eval_jaxpr/dot_general | solution.py:44
  58.6 4.0 %fusion.15 = f32[32,32,32]{2,1,0:T(8,128)S(1)} fusion(s32[256]{0:T(256)S(1)} %sub.67, s32[32,32]{1,0:T(8,128)S(1)} %iota_add_fusion.1, bf16[256,2,32,32]{0,3,2,1:T(8,128)(2,1)S(1)} %bitcast.97), kind=kOutput, calls=%fused_computation.44 | convolution fusion | flops 20709376 | bytes 672768 | tf_op jit(solution)/shard_map/while/body/eval_jaxpr/jal,ljb->jab/dot_general | solution.py:25
  62.6 4.0 %fusion.14 = f32[32,32,32]{2,1,0:T(8,128)S(1)} fusion(s32[256]{0:T(256)S(1)} %sub.67, s32[32,32]{1,0:T(8,128)S(1)} %iota_add_fusion.1, bf16[256,2,32,32]{0,3,2,1:T(8,128)(2,1)S(1)} %bitcast.98), kind=kOutput, calls=%fused_computation.43 | convolution fusion | flops 20709376 | bytes 672768 | tf_op jit(solution)/shard_map/while/body/eval_jaxpr/jal,ljb->jab/dot_general | solution.py:25
  66.6 0.0 copy-start.2
  66.6 4.3 %fusion.4 = f32[32,1,32,32]{3,2,0,1:T(8,128)S(1)} fusion(f32[32,32,32]{2,1,0:T(8,128)S(1)} %fusion.15, s32[256]{0:T(256)S(1)} %sub.67, s32[32,32]{1,0:T(8,128)S(1)} %iota_add_fusion.1, bf16[256,2,32,32]{0,3,2,1:T(8,128)(2,1)S(1)} %bitcast.99), kind=kOutput, calls=%fused_computation.22 | convolution fusion | flops 21004288 | bytes 1197056 | tf_op jit(solution)/shard_map/while/body/eval_jaxpr/jal,ljb->jab/dot_general | solution.py:25
  70.9 4.1 %fusion.3 = f32[32,1,32,32]{3,2,0,1:T(8,128)S(1)} fusion(f32[32,32,32]{2,1,0:T(8,128)S(1)} %fusion.14, s32[256]{0:T(256)S(1)} %sub.67, s32[32,32]{1,0:T(8,128)S(1)} %iota_add_fusion.1, bf16[256,2,32,32]{0,3,2,1:T(8,128)(2,1)S(1)} %bitcast.100), kind=kOutput, calls=%fused_computation.20 | convolution fusion | flops 21004288 | bytes 1197056 | tf_op jit(solution)/shard_map/while/body/eval_jaxpr/jal,ljb->jab/dot_general | solution.py:25
  75.0 0.0 copy-start.3
  75.0 0.0 copy-start.1
  75.0 0.1 pad_maximum_fusion.1
  75.1 0.1 copy.26
  75.2 1.2 %reshape.278 = f32[32,2048]{1,0:T(8,128)} reshape(f32[32,2,32,32]{3,2,1,0:T(8,128)S(1)} %copy.26) | data formatting | bytes 524288 | tf_op jit(solution)/shard_map/reshape | solution.py:71
  76.4 0.0 reduce-scatter.2.cloned.1.call-update
  76.4 0.1 broadcast_multiply_fusion
  76.5 0.0 copy-done.2
  76.5 14.6 %reduce-scatter.2.cloned.1.call-done = f32[16,2048]{1,0:T(8,128)} async-done(((f32[32,2048]{1,0:T(8,128)}), f32[16,2048]{1,0:T(8,128)}) %reduce-scatter.2.cloned.1.call-update) | async-done | bytes 131088 | tf_op jit(solution)/shard_map/reduce_scatter | solution.py:147
  91.1 1.1 reshape.279
  92.2 0.6 fusion.23
  92.8 0.6 fusion.22
  93.4 0.6 fusion.10
  94.0 0.6 fusion.46
  94.6 0.6 fusion.39
  95.2 0.6 fusion.9
  95.8 0.9 fusion.8
  96.6 0.6 multiply_add_fusion
  97.2 1.3 %fusion.18 = f32[16,32,128]{2,1,0:T(8,128)S(1)} fusion(f32[16,32,32]{2,1,0:T(8,128)S(1)} %get-tuple-element.27, f32[16,128]{1,0:T(8,128)S(1)} %get-tuple-element.33, f32[32]{0:T(128)S(1)} %iota_convert_fusion), kind=kOutput, calls=%fused_computation.56 | convolution fusion | flops 25296896 | bytes 336000 | tf_op jit(solution)/shard_map/jxy,jky->jxk/dot_general | solution.py:29
  98.6 1.3 %fusion.20 = f32[16,32,128]{2,1,0:T(8,128)S(1)} fusion(f32[16,32,32]{2,1,0:T(8,128)S(1)} %get-tuple-element.27, f32[16,128]{1,0:T(8,128)S(1)} %get-tuple-element.33, f32[32]{0:T(128)S(1)} %iota_convert_fusion), kind=kOutput, calls=%fused_computation.57 | convolution fusion | flops 25362432 | bytes 336000 | tf_op jit(solution)/shard_map/jxy,jky->jxk/dot_general | solution.py:29
  99.9 1.3 %fusion.6 = f32[16,128,32]{1,2,0:T(8,128)S(1)} fusion(f32[16,32,128]{2,1,0:T(8,128)S(1)} %fusion.18, f32[16,32,32]{2,1,0:T(8,128)S(1)} %get-tuple-element.26, f32[16,128]{1,0:T(8,128)S(1)} %get-tuple-element.33, f32[32]{0:T(128)S(1)} %iota_convert_fusion), kind=kOutput, calls=%fused_computation.26 | convolution fusion | flops 25427968 | bytes 598144 | tf_op jit(solution)/shard_map/jxy,jky->jxk/dot_general | solution.py:29
  101.2 2.4 %multiply_reduce_fusion.2 = (f32[16,128]{1,0:T(8,128)S(1)}, f32[16,128]{1,0:T(8,128)S(1)}, f32[16,128]{1,0:T(8,128)S(1)}, f32[16,128]{1,0:T(8,128)S(1)}) fusion(f32[32]{0:T(128)S(1)} %iota_convert_fusion, f32[16,128]{1,0:T(8,128)S(1)} %get-tuple-element.32, f32[16,128,32]{1,2,0:T(8,128)S(1)} %fusion.6, f32[16,32,128]{2,1,0:T(8,128)S(1)} %fusion.20, ...), kind=kOutput, calls=%fused_computation.49 | convolution fusion | flops 26075136 | bytes 639104 | tf_op jit(solution)/shard_map/jxy,jky->jxk/dot_general | solution.py:29
  103.6 0.6 copy.33
  104.2 3.3 %all-to-all-start = ((f32[2,4,4,128]{3,1,0,2:T(4,128)}), f32[2,4,4,128]{3,1,0,2:T(4,128)S(1)}, u32[]{:S(2)}, u32[]{:S(2)}) async-start(f32[2,4,4,128]{3,1,0,2:T(4,128)} %copy.33), calls=%async_computation.1 | async-start | bytes 32768 | tf_op jit(solution)/shard_map/all_to_all | solution.py:151
  107.5 0.0 copy-done.3
  107.5 0.1 broadcast_compare_fusion
  107.6 3.7 %all-to-all-done = f32[2,4,4,128]{3,1,0,2:T(4,128)S(1)} async-done(((f32[2,4,4,128]{3,1,0,2:T(4,128)}), f32[2,4,4,128]{3,1,0,2:T(4,128)S(1)}, u32[]{:S(2)}, u32[]{:S(2)}) %all-to-all-start) | async-done | bytes 16416 | tf_op jit(solution)/shard_map/all_to_all | solution.py:151
  111.3 0.0 copy-done.1
  111.4 0.6 copy.36
  (15 shorter events, 0.1 us)
Async XLA Ops:
  6.5 2.6 %copy-start = (f32[2,64,1024]{2,1,0:T(8,128)S(1)}, f32[2,64,1024]{2,1,0:T(8,128)}, u32[]{:S(2)}) copy-start(f32[2,64,1024]{2,1,0:T(8,128)} %param.8) | copy-start | bytes 1572868
  6.5 46.1 %all-gather.2.cloned.1.call-start = ((), (), s32[]{:S(2)}) async-start(), calls=%async_computation.2 | async-start | bytes 1310720 | tf_op jit(solution)/shard_map/all_gather | solution.py:140
  7.3 83.8 %reduce-scatter.2.cloned.1.call-start = ((), (), s32[]{:S(2)}) async-start(), calls=%async_computation.3 | async-start | bytes 393216 | tf_op jit(solution)/shard_map/reduce_scatter | solution.py:147
  66.6 9.9 %copy-start.2 = (f32[2,16,128]{2,1,0:T(8,128)S(1)}, f32[2,16,128]{2,1,0:T(8,128)}, u32[]{:S(2)}) copy-start(f32[2,16,128]{2,1,0:T(8,128)} %param.11) | copy-start | bytes 49156
  75.0 32.5 %copy-start.3 = (s32[4,1]{0,1:T(1,128)S(1)}, s32[4,1]{0,1:T(1,128)}, u32[]{:S(2)}) copy-start(s32[4,1]{0,1:T(1,128)} %param.13) | copy-start | bytes 52
  75.0 36.3 %copy-start.1 = (f32[2,4,1,512]{3,2,1,0:T(1,128)S(1)}, f32[2,4,1,512]{3,2,1,0:T(1,128)}, u32[]{:S(2)}) copy-start(f32[2,4,1,512]{3,2,1,0:T(1,128)} %param.12) | copy-start | bytes 49156
  104.2 7.1 %all-to-all-start = ((f32[2,4,4,128]{3,1,0,2:T(4,128)}), f32[2,4,4,128]{3,1,0,2:T(4,128)S(1)}, u32[]{:S(2)}, u32[]{:S(2)}) async-start(f32[2,4,4,128]{3,1,0,2:T(4,128)} %copy.33), calls=%async_computation.1 | async-start | bytes 32768 | tf_op jit(solution)/shard_map/all_to_all | solution.py:151
Sparse Core Ops, SparseCore 0:
  8.9 30.7 all-gather.1
  76.6 14.4 reduce-scatter.1
where the time goes:
time: 119 us
  other arithmetic  43 us (36%)
  matrix products  33.7 us (28%)
  waiting for transfers between devices  19 us (16%)
  between operations  13.6 us (11%)
  local copies, waits for them, and re-layouts  6.18 us (5%)
  starting transfers between devices  3.3 us (3%)
    another operation x1, other arithmetic  35.5 us
    dot_general x4, matrix products, narrow_mix(): return jnp.einsum(pattern, left, right, preferred_element_type=jnp.float32)  16.4 us
    reduce_scatter x1, waiting for transfers between devices, on_device(): lax.psum_scatter(group_cuts, 'tile', scatter_dimension=0, tiled=True)  14.6 us
    dot_general x12, matrix products, exact_mix(): return jnp.einsum(pattern, left, right, precision=lax.Precision.HIGHEST)  11.3 us
    another operation x1, other arithmetic, tile_cuts(): jnp.stack([ev_real, ev_imag], axis=1).reshape(columns, 2 * block_size * SG)  6.18 us
    dot_general x1, matrix products, tile_cuts(): jnp.dot(strip_rows, phase_table, preferred_element_type=jnp.float32)  6 us
    all_to_all x1, waiting for transfers between devices, on_device(): lax.all_to_all(outgoing, 'chan', split_axis=2, concat_axis=3, tiled=True)  3.74 us
    all_to_all x1, starting transfers between devices, on_device(): lax.all_to_all(outgoing, 'chan', split_axis=2, concat_axis=3, tiled=True)  3.25 us
  transfers between devices with their start and end apart: 3, of which 2 were waited for; matrix products, arithmetic and copies ran while one was open for 38% of the time, Pallas kernels for 0%

commit v1 on v0

--- a/solution.py
+++ b/solution.py
@@ -1,8 +1,11 @@
+import functools
 import math
 
 import jax
 import jax.numpy as jnp
 from jax import lax
+from jax.experimental import pallas as pl
+from jax.experimental.pallas import tpu as pltpu
 from jax.sharding import PartitionSpec as P
 
 SG = 32
@@ -11,8 +14,9 @@
 TILE_DEV = 4
 TL = 64
 SUB_TILE = 16
-
-
+PACK = 4
+
+MESH = pl.DeviceIdType.MESH
 two_pi = 6.283185307179586
 
 
@@ -21,54 +25,229 @@
     return (jnp.cos(angle_turns), -jnp.sin(angle_turns))
 
 
-def narrow_mix(pattern, left, right):
-    return jnp.einsum(pattern, left, right, preferred_element_type=jnp.float32)
+def octant_polys(theta):
+    z = theta * theta
+    s = theta + theta * z * (
+        -1.6666654611e-1 + z * (8.3321608736e-3 + z * -1.9515295891e-4)
+    )
+    c = 1.0 - 0.5 * z + z * z * (
+        4.166664568298827e-2 + z * (-1.388731625493765e-3 + z * 2.443315711809948e-5)
+    )
+    return s, c
+
+
+def turn_quadrant(quadrant, s, c):
+    odd = (quadrant & 1) == 1
+    cos_part = jnp.where(odd, s, c)
+    sin_part = jnp.where(odd, c, s)
+    cos_part = jnp.where(((quadrant + 1) & 2) == 2, -cos_part, cos_part)
+    sin_part = jnp.where((quadrant & 2) == 2, sin_part, -sin_part)
+    return cos_part, sin_part
+
+
+def unit_phase(products):
+    k = products & (NG - 1)
+    quadrant = (k + NG // 8) >> (NG.bit_length() - 3)
+    theta = (k - quadrant * (NG // 4)).astype(jnp.float32) * (two_pi / NG)
+    s, c = octant_polys(theta)
+    return turn_quadrant(quadrant, s, c)
+
+
+def cmul(ar, ai, br, bi):
+    return ar * br - ai * bi, ar * bi + ai * br
+
+
+def dot_nt(a, b):
+    return lax.dot_general(a, b, (((1,), (1,)), ((), ())), preferred_element_type=jnp.float32)
+
+
+def remote(src, dst, send, recv, where):
+    return pltpu.make_async_remote_copy(
+        src_ref=src, dst_ref=dst, send_sem=send, recv_sem=recv, device_id=where, device_id_type=MESH
+    )
+
+
+def cuts_kernel(
+    n_stn, n_chan, n_tile,
+    x_ref, off_ref, out_ref,
+    full, ar, ai, br, bi, cr, ci, dr, di, tab, eu, cuts, inbox,
+    z_send, y_send, m_send, recv, cut_send, cut_recv,
+):
+    stn, chan, tile = lax.axis_index("stn"), lax.axis_index("chan"), lax.axis_index("tile")
+    tiles, piece_rows, columns = x_ref.shape
+    quarter = columns // n_chan
+    rows = n_stn * tiles * piece_rows
+    group = SUB_TILE * n_tile
+    strip_half = TILE_DEV * n_tile * TL // 2
+    mate, across = chan ^ 1, chan ^ 2
+    hops = [1, n_stn - 1] + list(range(2, n_stn - 1))
+    sources = [lax.rem(stn + d, n_stn) for d in hops]
+
+    barrier = pltpu.get_barrier_semaphore()
+    partners = [{"stn": s} for s in sources] + [{"chan": mate}, {"chan": across}]
+    partners += [{"tile": lax.rem(tile + d, n_tile)} for d in range(1, n_tile)]
+    for where in partners:
+        pl.semaphore_signal(barrier, inc=1, device_id=where, device_id_type=MESH)
+    pl.semaphore_wait(barrier, len(partners))
+
+    own = x_ref.at[:, :, pl.ds(pl.multiple_of(chan * quarter, quarter), quarter)]
+    z_copies = [
+        remote(own, full.at[chan, stn], z_send.at[n], recv.at[chan, stn], {"stn": s})
+        for n, s in enumerate(sources)
+    ]
+    for copy in z_copies:
+        copy.start()
+    for c in range(n_chan):
+        full[c, stn] = x_ref[:, :, c * quarter:(c + 1) * quarter]
+
+    first = pl.multiple_of(stn * group, group)
+    col_pos = lax.broadcasted_iota(jnp.int32, (8, columns), 1) - columns // 2
+    lane = lax.broadcasted_iota(jnp.int32, (8, rows), 1)
+    shard = tiles * piece_rows
+    row_s = lax.div(lane, shard)
+    row_t = lax.div(lax.rem(lane, shard), piece_rows)
+    row_pos = (tile * TILE_DEV + row_t) * TL + row_s * piece_rows + lax.rem(lane, piece_rows) - strip_half
+    for step in range(SG // 8):
+        part = slice(8 * step, 8 * step + 8)
+        pixel = lax.broadcasted_iota(jnp.int32, (8, 1), 0) + 8 * step
+        br[part], bi[part] = unit_phase(pixel * col_pos)
+        dr[part], di[part] = unit_phase(pixel * row_pos)
+
+    @pl.loop(0, group // 8)
+    def _(step):
+        at = pl.multiple_of(step * 8, 8)
+        corners = off_ref[pl.ds(first + at, 8), :]
+        ar[pl.ds(at, 8)], ai[pl.ds(at, 8)] = unit_phase(corners[:, 1:2] * col_pos)
+        cr[pl.ds(at, 8)], ci[pl.ds(at, 8)] = unit_phase(corners[:, 0:1] * row_pos)
+
+    @pl.loop(0, group // PACK)
+    def _(pack):
+        base = pl.multiple_of(pack * 2 * PACK * SG, 2 * PACK * SG)
+        for n in range(PACK):
+            j = pack * PACK + n
+            real, imag = cmul(ar[pl.ds(j, 1)], ai[pl.ds(j, 1)], br[...], bi[...])
+            tab[pl.ds(base + n * SG, SG)] = real.astype(jnp.bfloat16)
+            tab[pl.ds(base + (PACK + n) * SG, SG)] = imag.astype(jnp.bfloat16)
+            real, imag = cmul(cr[pl.ds(j, 1)], ci[pl.ds(j, 1)], dr[...], di[...])
+            real, imag = real.astype(jnp.bfloat16), imag.astype(jnp.bfloat16)
+            eu[pl.ds(base + n * SG, SG), :rows] = real
+            eu[pl.ds(base + n * SG, SG), rows:] = -imag
+            eu[pl.ds(base + (PACK + n) * SG, SG), :rows] = imag
+            eu[pl.ds(base + (PACK + n) * SG, SG), rows:] = real
+
+    onward = []
+    for n, s in enumerate(sources):
+        piece = full.at[chan, s]
+        remote(own, piece, z_send.at[n], recv.at[chan, s], {"stn": s}).wait_recv()
+        for sems, slot, where in ((y_send, n, across), (m_send, n, mate)):
+            copy = remote(piece, piece, sems.at[slot], recv.at[chan, s], {"chan": where})
+            copy.start()
+            onward.append(copy)
+    for n, s in enumerate(sources):
+        piece = full.at[across, s]
+        remote(piece, piece, y_send.at[n], recv.at[across, s], {"chan": across}).wait_recv()
+        copy = remote(piece, piece, m_send.at[len(sources) + n], recv.at[across, s], {"chan": mate})
+        copy.start()
+        onward.append(copy)
+    for n, s in enumerate(sources):
+        for c in (mate, mate ^ 2):
+            piece = full.at[c, s]
+            remote(piece, piece, y_send.at[n], recv.at[c, s], {"chan": mate}).wait_recv()
+    for copy in z_copies + onward:
+        copy.wait_send()
+
+    lane_pack = lax.broadcasted_iota(jnp.int32, (SG, PACK * SG), 1) >> (SG.bit_length() - 1)
+
+    def own_block(half):
+        picked = half[:SG]
+        for n in range(1, PACK):
+            picked = jnp.where(lane_pack == n, half[n * SG:(n + 1) * SG], picked)
+        return picked
+
+    packs = SUB_TILE // PACK
+    both = 2 * PACK * SG
+    per_step = 2
+    sent = []
+    for d in range(1, n_tile + 1):
+        peer = lax.rem(tile + d, n_tile)
+
+        @pl.loop(0, packs // per_step)
+        def _(step):
+            pack = peer * packs + step * per_step
+            at = pl.multiple_of(pack * both, both)
+            q = dot_nt(tab[pl.ds(at, per_step * both), :quarter], full[0].reshape(rows, quarter))
+            for c in range(1, n_chan):
+                q += dot_nt(
+                    tab[pl.ds(at, per_step * both), c * quarter:(c + 1) * quarter],
+                    full[c].reshape(rows, quarter),
+                )
+            q = q.astype(jnp.bfloat16)
+            for k in range(per_step):
+                top = k * both
+                q_k = jnp.concatenate(
+                    [q[top:top + both // 2], q[top + both // 2:top + both]], axis=1
+                )
+                cut = dot_nt(eu[pl.ds(at + top, both)], q_k)
+                cuts[pack + k, :SG] = own_block(cut[:both // 2])
+                cuts[pack + k, SG:] = own_block(cut[both // 2:])
+
+        if d < n_tile:
+            copy = remote(
+                cuts.at[pl.ds(peer * packs, packs)], inbox.at[d - 1],
+                cut_send.at[d - 1], cut_recv.at[d - 1], {"tile": peer},
+            )
+            copy.start()
+            sent.append(copy)
+    total = cuts[pl.ds(tile * packs, packs)]
+    for d, copy in enumerate(sent):
+        copy.wait()
+        total += inbox[d]
+    out_ref[...] = total
+
+
+def own_cuts_call(model_image, offsets):
+    n_stn, n_chan, n_tile = (lax.axis_size(a) for a in ("stn", "chan", "tile"))
+    tiles, piece_rows, columns = model_image.shape
+    rows = n_stn * tiles * piece_rows
+    group = SUB_TILE * n_tile
+    packs = SUB_TILE // PACK
+    f32, bf16 = jnp.float32, jnp.bfloat16
+    vmem = pl.BlockSpec(memory_space=pltpu.VMEM)
+    dma = pltpu.SemaphoreType.DMA
+    return pl.pallas_call(
+        functools.partial(cuts_kernel, n_stn, n_chan, n_tile),
+        out_shape=jax.ShapeDtypeStruct((packs, 2 * SG, PACK * SG), f32),
+        in_specs=[vmem, vmem],
+        out_specs=vmem,
+        scratch_shapes=[
+            pltpu.VMEM((n_chan, n_stn, tiles, piece_rows, columns // n_chan), bf16),
+            pltpu.VMEM((group, columns), f32),
+            pltpu.VMEM((group, columns), f32),
+            pltpu.VMEM((SG, columns), f32),
+            pltpu.VMEM((SG, columns), f32),
+            pltpu.VMEM((group, rows), f32),
+            pltpu.VMEM((group, rows), f32),
+            pltpu.VMEM((SG, rows), f32),
+            pltpu.VMEM((SG, rows), f32),
+            pltpu.VMEM((group * 2 * SG, columns), bf16),
+            pltpu.VMEM((group * 2 * SG, 2 * rows), bf16),
+            pltpu.VMEM((group // PACK, 2 * SG, PACK * SG), f32),
+            pltpu.VMEM((max(n_tile - 1, 1), packs, 2 * SG, PACK * SG), f32),
+            dma((n_stn - 1,)),
+            dma((n_stn - 1,)),
+            dma((2 * (n_stn - 1),)),
+            dma((n_chan, n_stn)),
+            dma((max(n_tile - 1, 1),)),
+            dma((max(n_tile - 1, 1),)),
+        ],
+        compiler_params=pltpu.CompilerParams(
+            collective_id=0, has_side_effects=True, vmem_limit_bytes=60 * 1024 * 1024
+        ),
+    )(model_image, offsets)
 
 
 def exact_mix(pattern, left, right):
     return jnp.einsum(pattern, left, right, precision=lax.Precision.HIGHEST)
-
-
-def tile_cuts(strip_rows, row_ids, offset_block, strip_half):
-    block_size = offset_block.shape[0]
-    columns = strip_rows.shape[1]
-    pixel_idx = jnp.arange(SG, dtype=jnp.int32)
-    col_pos = jnp.arange(columns, dtype=jnp.int32) - columns // 2
-    v_index = offset_block[:, 1][:, None] + pixel_idx[None, :]
-    ev_real, ev_imag = phase_pair(col_pos[:, None, None] * v_index[None, :, :], NG)
-    phase_table = (
-        jnp.stack([ev_real, ev_imag], axis=1)
-        .reshape(columns, 2 * block_size * SG)
-        .astype(jnp.bfloat16)
-    )
-    partial_q = jnp.dot(strip_rows, phase_table, preferred_element_type=jnp.float32).astype(
-        jnp.bfloat16
-    )
-    partial_q = partial_q.reshape(strip_rows.shape[0], 2, block_size, SG)
-    q_real = partial_q[:, 0]
-    q_imag = partial_q[:, 1]
-    u_index = offset_block[:, 0][:, None] + pixel_idx[None, :]
-    row_pos = row_ids - strip_half
-    eu_real, eu_imag = phase_pair(u_index[:, :, None] * row_pos[None, None, :], NG)
-    eu_real = eu_real.astype(jnp.bfloat16)
-    eu_imag = eu_imag.astype(jnp.bfloat16)
-    cut_real = narrow_mix("jal,ljb->jab", eu_real, q_real) - narrow_mix(
-        "jal,ljb->jab", eu_imag, q_imag
-    )
-    cut_imag = narrow_mix("jal,ljb->jab", eu_real, q_imag) + narrow_mix(
-        "jal,ljb->jab", eu_imag, q_real
-    )
-    return jnp.stack([cut_real, cut_imag], axis=1).reshape(block_size, 2 * SG * SG)
-
-
-def cuts_blocked(strip_rows, row_ids, offsets, strip_half):
-    how_many = offsets.shape[0]
-    block_size = math.gcd(how_many, 32)
-    grouped = offsets.reshape(how_many // block_size, block_size, 2)
-    stacked = lax.map(
-        lambda offset_block: tile_cuts(strip_rows, row_ids, offset_block, strip_half), grouped
-    )
-    return stacked.reshape(how_many, 2 * SG * SG)
 
 
 def predict(cut_rows, pair_ids, station_beams, uv_block):
@@ -128,23 +307,9 @@
     observed,
     live_counts,
 ):
-    tile_count = lax.axis_size("tile")
-    columns = model_image.shape[2]
-    strip_half = TILE_DEV * tile_count * TL // 2
-    group_offsets = subgrid_offsets[0]
-    stn_index = lax.axis_index("stn")
-    tile_first = lax.axis_index("tile") * TILE_DEV
-    tile_ids = jnp.arange(TILE_DEV, dtype=jnp.int32)
-    group_size = SUB_TILE * tile_count
-    station_offsets = lax.dynamic_slice_in_dim(group_offsets, stn_index * group_size, group_size, 0)
-    shard_piece = lax.all_gather(model_image, "stn", axis=1, tiled=True)
-    piece_rows = shard_piece.shape[1]
-    piece_ids = (
-        (tile_first + tile_ids)[:, None] * TL + jnp.arange(piece_rows, dtype=jnp.int32)[None, :]
-    ).reshape(-1)
-    piece_strip = shard_piece.reshape(TILE_DEV * piece_rows, columns)
-    group_cuts = cuts_blocked(piece_strip, piece_ids, station_offsets, strip_half)
-    own_cuts = lax.psum_scatter(group_cuts, "tile", scatter_dimension=0, tiled=True)
+    packed = own_cuts_call(model_image, subgrid_offsets[0])
+    own_cuts = packed.reshape(SUB_TILE // PACK, 2, SG, PACK, SG).transpose(0, 3, 1, 2, 4)
+    own_cuts = own_cuts.reshape(SUB_TILE, 2 * SG * SG)
     predicted = predict(own_cuts, subgrid_stations, station_beams, visibility_uv)
     chan_count = lax.axis_size("chan")
     outgoing = predicted.reshape(2, SUB_TILE // chan_count, chan_count, predicted.shape[2])

time: 119 us -> 52.9 us (0.44)
  other arithmetic: 43 us -> 0.22 us
  Pallas kernels: 0 us -> 27.3 us
  matrix products: 33.7 us -> 10.4 us
  waiting for transfers between devices: 19 us -> 3.08 us
  between operations: 13.6 us -> 0.23 us
  local copies, waits for them, and re-layouts: 6.18 us -> 8.02 us
    another operation x3 -> x0, other arithmetic: 41.7 us -> none
    pallas_call x0 -> x1, Pallas kernels: none -> 27.3 us  [own_cuts_call(): pl.pallas_call(functools.partial(cuts_kernel, n_stn, n_chan, n_tile), out...]
    dot_general x5 -> x0, matrix products: 22.4 us -> none  [the longest x4 16.4 us: narrow_mix(): return jnp.einsum(pattern, left, right, preferred_element_type=jnp.float32)]
    reduce_scatter x1 -> x0, waiting for transfers between devices: 14.6 us -> none  [on_device(): lax.psum_scatter(group_cuts, 'tile', scatter_dimension=0, tiled=True)]
    unnamed x8 -> x11, local copies, waits for them, and re-layouts: 0.02 us -> 3.69 us
  transfers between devices with their start and end apart: 3 -> 1, of which waited for: 2 -> 1; matrix products, arithmetic and copies ran while one was open for 38% -> 0% of each run, Pallas kernels for 0% -> 0%
where the time goes in v1:
time: 52.9 us; the launch traced here: 52.5 us
  Pallas kernels  27.3 us (52%)
  matrix products  10.4 us (20%)
  local copies, waits for them, and re-layouts  8.02 us (15%)
  starting transfers between devices  3.25 us (6%)
  waiting for transfers between devices  3.08 us (6%)
    pallas_call x1, Pallas kernels, own_cuts_call(): pl.pallas_call(functools.partial(cuts_kernel, n_stn, n_chan, n_tile), out...  27.3 us
    dot_general x12, matrix products, exact_mix(): return jnp.einsum(pattern, left, right, precision=lax.Precision.HIGHEST)  10.4 us
    unnamed x11, local copies, waits for them, and re-layouts  3.69 us
    all_to_all x1, starting transfers between devices, on_device(): lax.all_to_all(outgoing, 'chan', split_axis=2, concat_axis=3, tiled=True)  3.25 us
    all_to_all x1, waiting for transfers between devices, on_device(): lax.all_to_all(outgoing, 'chan', split_axis=2, concat_axis=3, tiled=True)  3.08 us
    reshape x1, local copies, waits for them, and re-layouts, on_device(): packed.reshape(SUB_TILE // PACK, 2, SG, PACK, SG).transpose(0, 3, 1, 2, 4)  1.16 us
  transfers between devices with their start and end apart: 1, of which 1 were waited for; matrix products, arithmetic and copies ran while one was open for 0% of the time, Pallas kernels for 0%

profile of v1, /device:TPU:0, one launch (start us, length us, event | category | flops | bytes accessed | tf_op | source)
XLA Modules:
  0.0 52.5 jit_solution(13153216634317282897)
XLA Ops:
  0.0 0.0 copy-start
  0.0 1.5 %copy.26 = s32[1,128,2]{2,1,0:T(8,128)} copy(s32[1,128,2]{1,2,0:T(2,128)} %param.9) | data formatting | bytes 2048 | tf_op args[2]
  1.5 27.3 %shard_map.73 = f32[4,64,128]{2,1,0:T(8,128)} custom-call(bf16[4,16,2048]{2,1,0:T(8,128)(2,1)} %x_ref.1, s32[128,2]{1,0:T(8,128)} %bitcast.69), custom_call_target="tpu_custom_call" | custom-call | tf_op jit(solution)/shard_map/pallas_call | solution.py:217
  28.7 1.2 %reshape.130 = f32[4,2,32,4,32]{4,3,2,1,0:T(4,128)S(1)} reshape(f32[4,64,128]{2,1,0:T(8,128)} %shard_map.73) | data formatting | bytes 262144 | tf_op jit(solution)/shard_map/reshape | solution.py:311
  29.9 0.2 copy.27
  30.1 0.4 fusion.13
  30.6 0.4 fusion.12
  31.0 0.4 fusion.5
  31.4 0.6 %fusion.36 = f32[16,32,32]{2,1,0:T(8,128)S(1)} fusion(f32[16,32,32]{1,2,0:T(8,128)S(1)} %fusion.5), kind=kOutput, calls=%fused_computation.60 | convolution fusion | flops 6305792 | bytes 131072 | tf_op jit(solution)/shard_map/jxb,yb->jxy/dot_general | solution.py:250
  32.0 0.6 %fusion.29 = f32[16,32,32]{2,1,0:T(8,128)S(1)} fusion(f32[16,32,32]{1,2,0:T(8,128)S(1)} %fusion.5), kind=kOutput, calls=%fused_computation.53 | convolution fusion | flops 6305792 | bytes 131072 | tf_op jit(solution)/shard_map/jxb,yb->jxy/dot_general | solution.py:250
  32.7 0.0 copy-start.3
  32.7 0.4 fusion.4
  33.1 0.2 copy-done.3
  33.4 0.0 copy-done
  33.4 0.7 %gather_fusion = f32[16,2,1024]{2,0,1:T(8,128)S(1)} fusion(f32[2,64,1024]{2,1,0:T(8,128)S(1)} %copy-done, s32[1024]{0:T(1024)S(1)} %get-tuple-element.20), kind=kCustom, calls=%fused_computation | custom fusion | bytes 262208 | tf_op jit(solution)/shard_map/gather | solution.py:272
  34.1 0.7 %gather_fusion.1 = f32[16,2,1024]{2,0,1:T(8,128)S(1)} fusion(f32[2,64,1024]{2,1,0:T(8,128)S(1)} %copy-done, s32[1024]{0:T(1024)S(1)} %get-tuple-element.19), kind=kCustom, calls=%fused_computation.1 | custom fusion | bytes 262208 | tf_op jit(solution)/shard_map/gather | solution.py:273
  34.9 0.1 add.81
  35.0 0.1 sub.59
  35.1 0.0 copy-start.2
  35.1 0.1 broadcast_multiply_fusion
  35.2 0.6 %copy-done.2 = f32[2,16,128]{2,1,0:T(8,128)S(1)} copy-done((f32[2,16,128]{2,1,0:T(8,128)S(1)}, f32[2,16,128]{2,1,0:T(8,128)}, u32[]{:S(2)}) %copy-start.2) | copy-done | bytes 16408
  35.9 0.6 %fusion.3 = f32[16,32,32]{2,1,0:T(8,128)S(1)} fusion(f32[16,32,32]{2,1,0:T(8,128)S(1)} %fusion.36, f32[16,32,32]{1,2,0:T(8,128)S(1)} %fusion.4), kind=kOutput, calls=%fused_computation.9 | convolution fusion | flops 6338560 | bytes 196608 | tf_op jit(solution)/shard_map/jxb,yb->jxy/dot_general | solution.py:250
  36.5 0.6 %multiply_add_fusion = (f32[16,32,32]{2,1,0:T(8,128)S(1)}, f32[16,32,32]{2,1,0:T(8,128)S(1)}) fusion(f32[16,32,32]{2,1,0:T(8,128)S(1)} %fusion.3, f32[16,32,32]{2,1,0:T(8,128)S(1)} %sub.59, f32[16,32,32]{2,1,0:T(8,128)S(1)} %add.81, f32[32,32]{1,0:T(8,128)S(1)} %broadcast_multiply_fusion, f32[16,32,32]{2,1,0:T(8,128)S(1)} %fusion.29, ...), kind=kOutput, calls=%fused_computation.22 | convolution fusion | flops 6469632 | bytes 462848 | tf_op jit(solution)/shard_map/jxb,yb->jxy/dot_general | solution.py:250
  37.1 1.3 %fusion.8 = f32[16,32,128]{2,1,0:T(8,128)S(1)} fusion(f32[16,32,32]{2,1,0:T(8,128)S(1)} %get-tuple-element.12, f32[16,128]{1,0:T(8,128)S(1)} %get-tuple-element.16, f32[32]{0:T(128)S(1)} %iota_convert_fusion), kind=kOutput, calls=%fused_computation.25 | convolution fusion | flops 25296896 | bytes 336000 | tf_op jit(solution)/shard_map/jxy,jky->jxk/dot_general | solution.py:250
  38.4 1.3 %fusion.10 = f32[16,32,128]{2,1,0:T(8,128)S(1)} fusion(f32[16,32,32]{2,1,0:T(8,128)S(1)} %get-tuple-element.12, f32[16,128]{1,0:T(8,128)S(1)} %get-tuple-element.16, f32[32]{0:T(128)S(1)} %iota_convert_fusion), kind=kOutput, calls=%fused_computation.26 | convolution fusion | flops 25362432 | bytes 336000 | tf_op jit(solution)/shard_map/jxy,jky->jxk/dot_general | solution.py:250
  39.7 1.3 %fusion.1 = f32[16,128,32]{1,2,0:T(8,128)S(1)} fusion(f32[16,32,128]{2,1,0:T(8,128)S(1)} %fusion.8, f32[16,32,32]{2,1,0:T(8,128)S(1)} %get-tuple-element.11, f32[16,128]{1,0:T(8,128)S(1)} %get-tuple-element.16, f32[32]{0:T(128)S(1)} %iota_convert_fusion), kind=kOutput, calls=%fused_computation.5 | convolution fusion | flops 25427968 | bytes 598144 | tf_op jit(solution)/shard_map/jxy,jky->jxk/dot_general | solution.py:250
  41.0 2.4 %multiply_reduce_fusion.2 = (f32[16,128]{1,0:T(8,128)S(1)}, f32[16,128]{1,0:T(8,128)S(1)}, f32[16,128]{1,0:T(8,128)S(1)}, f32[16,128]{1,0:T(8,128)S(1)}) fusion(f32[32]{0:T(128)S(1)} %iota_convert_fusion, f32[16,128]{1,0:T(8,128)S(1)} %get-tuple-element.15, f32[16,128,32]{1,2,0:T(8,128)S(1)} %fusion.1, f32[16,32,128]{2,1,0:T(8,128)S(1)} %fusion.10, ...), kind=kOutput, calls=%fused_computation.18 | convolution fusion | flops 26075136 | bytes 639104 | tf_op jit(solution)/shard_map/jxy,jky->jxk/dot_general | solution.py:250
  43.4 0.6 %copy.32 = f32[2,4,4,128]{3,1,0,2:T(4,128)} copy(f32[2,4,4,128]{3,2,1,0:T(4,128)S(1)} %pad_maximum_fusion) | data formatting | bytes 32768 | tf_op jit(solution)/shard_map/stack | solution.py:298
  44.1 3.3 %all-to-all-start = ((f32[2,4,4,128]{3,1,0,2:T(4,128)}), f32[2,4,4,128]{3,1,0,2:T(4,128)S(1)}, u32[]{:S(2)}, u32[]{:S(2)}) async-start(f32[2,4,4,128]{3,1,0,2:T(4,128)} %copy.32), calls=%async_computation | async-start | bytes 32768 | tf_op jit(solution)/shard_map/all_to_all | solution.py:316
  47.3 0.0 copy-start.4
  47.3 0.6 %copy-done.4 = s32[4,1]{0,1:T(1,128)S(1)} copy-done((s32[4,1]{0,1:T(1,128)S(1)}, s32[4,1]{0,1:T(1,128)}, u32[]{:S(2)}) %copy-start.4) | copy-done | bytes 40
  48.0 0.1 broadcast_compare_fusion
  48.1 3.1 %all-to-all-done = f32[2,4,4,128]{3,1,0,2:T(4,128)S(1)} async-done(((f32[2,4,4,128]{3,1,0,2:T(4,128)}), f32[2,4,4,128]{3,1,0,2:T(4,128)S(1)}, u32[]{:S(2)}, u32[]{:S(2)}) %all-to-all-start) | async-done | bytes 16416 | tf_op jit(solution)/shard_map/all_to_all | solution.py:316
  51.2 0.0 copy-start.1
  51.2 0.7 %copy-done.1 = f32[2,4,1,512]{3,2,1,0:T(1,128)S(1)} copy-done((f32[2,4,1,512]{3,2,1,0:T(1,128)S(1)}, f32[2,4,1,512]{3,2,1,0:T(1,128)}, u32[]{:S(2)}) %copy-start.1) | copy-done | bytes 16408
  51.9 0.6 %copy.35 = f32[2,4,1,512]{3,2,1,0:T(1,128)} copy(f32[2,4,1,512]{3,1,0,2:T(4,128)S(1)} %fusion.39) | data formatting | bytes 32768 | tf_op jit(solution)/shard_map/jit(_where)/select_n | solution.py:320
  (13 shorter events, 0.1 us)
Async XLA Ops:
  0.0 33.4 %copy-start = (f32[2,64,1024]{2,1,0:T(8,128)S(1)}, f32[2,64,1024]{2,1,0:T(8,128)}, u32[]{:S(2)}) copy-start(f32[2,64,1024]{2,1,0:T(8,128)} %param.8) | copy-start | bytes 1572868
  32.7 0.7 %copy-start.3 = (s32[16,2]{0,1:T(2,128)S(1)}, s32[16,2]{0,1:T(2,128)}, u32[]{:S(2)}) copy-start(s32[16,2]{0,1:T(2,128)} %param.10) | copy-start | bytes 388
  35.1 0.7 %copy-start.2 = (f32[2,16,128]{2,1,0:T(8,128)S(1)}, f32[2,16,128]{2,1,0:T(8,128)}, u32[]{:S(2)}) copy-start(f32[2,16,128]{2,1,0:T(8,128)} %param.11) | copy-start | bytes 49156
  44.1 7.1 %all-to-all-start = ((f32[2,4,4,128]{3,1,0,2:T(4,128)}), f32[2,4,4,128]{3,1,0,2:T(4,128)S(1)}, u32[]{:S(2)}, u32[]{:S(2)}) async-start(f32[2,4,4,128]{3,1,0,2:T(4,128)} %copy.32), calls=%async_computation | async-start | bytes 32768 | tf_op jit(solution)/shard_map/all_to_all | solution.py:316
  47.3 0.7 %copy-start.4 = (s32[4,1]{0,1:T(1,128)S(1)}, s32[4,1]{0,1:T(1,128)}, u32[]{:S(2)}) copy-start(s32[4,1]{0,1:T(1,128)} %param.13) | copy-start | bytes 52
  51.2 0.7 %copy-start.1 = (f32[2,4,1,512]{3,2,1,0:T(1,128)S(1)}, f32[2,4,1,512]{3,2,1,0:T(1,128)}, u32[]{:S(2)}) copy-start(f32[2,4,1,512]{3,2,1,0:T(1,128)} %param.12) | copy-start | bytes 49156

commit v2 on v1

--- a/solution.py
+++ b/solution.py
@@ -1,5 +1,4 @@
 import functools
-import math
 
 import jax
 import jax.numpy as jnp
@@ -20,11 +19,6 @@
 two_pi = 6.283185307179586
 
 
-def phase_pair(products, modulus):
-    angle_turns = jnp.mod(products, modulus).astype(jnp.float32) * (two_pi / modulus)
-    return (jnp.cos(angle_turns), -jnp.sin(angle_turns))
-
-
 def octant_polys(theta):
     z = theta * theta
     s = theta + theta * z * (
@@ -53,6 +47,31 @@
     return turn_quadrant(quadrant, s, c)
 
 
+def turn_fraction(turns):
+    quadrant = jnp.floor(turns * (4.0 / SG) + 0.5)
+    theta = (turns - quadrant * (SG / 4.0)) * (two_pi / SG)
+    s, c = octant_polys(theta)
+    return turn_quadrant(quadrant.astype(jnp.int32), s, c)
+
+
+def dft_entries(out_part, out_pixel, in_part, in_pixel):
+    turns = out_pixel * in_pixel + (SG // 4) * (in_part - out_part)
+    return unit_phase(turns * (NG // SG))[0]
+
+
+def split(x):
+    high = x.astype(jnp.bfloat16)
+    return high, (x - high.astype(jnp.float32)).astype(jnp.bfloat16)
+
+
+def dot_nn(a, b):
+    return jnp.dot(a, b, preferred_element_type=jnp.float32)
+
+
+def iota(shape, axis):
+    return lax.broadcasted_iota(jnp.int32, shape, axis)
+
+
 def cmul(ar, ai, br, bi):
     return ar * br - ai * bi, ar * bi + ai * br
 
@@ -67,11 +86,87 @@
     )
 
 
-def cuts_kernel(
+def prediction_tables(pair_ref, beam_ref, uv_ref, beams, gain, dft_x, dft_y, ev, uu):
+    log_sg, half = SG.bit_length() - 1, PACK * SG
+    rows_at = SG // PACK
+    packs = SUB_TILE // PACK
+
+    shape = (2 * SG, 6 * SG)
+    row, col = iota(shape, 0), iota(shape, 1)
+    line = row & (SG - 1)
+    x = PACK * (line & (rows_at - 1)) + line // rows_at
+    entries = dft_entries(row >> log_sg, x, (col >> log_sg) & 1, col & (SG - 1))
+    high, low = split(entries)
+    dft_x[...] = jnp.where(col >= 4 * SG, low.astype(jnp.float32), high.astype(jnp.float32)).astype(
+        jnp.bfloat16
+    )
+
+    shape = (half, 2 * half)
+    for part in range(2):
+        row, col = iota(shape, 0), iota(shape, 1)
+        out_part = (col >= half).astype(jnp.int32)
+        entries = dft_entries(out_part, col & (SG - 1), part, row & (SG - 1))
+        same = (row >> log_sg) == ((col >> log_sg) & (PACK - 1))
+        high, low = split(jnp.where(same, entries * (1.0 / (SG * SG)), 0.0))
+        dft_y[0, part * half:(part + 1) * half] = high
+        dft_y[1, part * half:(part + 1) * half] = low
+
+    @pl.loop(0, SUB_TILE)
+    def _(j):
+        for side in range(2):
+            station = pair_ref[side, j]
+            for part in range(2):
+                flat = beam_ref[part, pl.ds(station, 1)]
+                for c in range(rows_at):
+                    beams[side, part, j, c:c + 1] = flat[:, c * half:(c + 1) * half]
+
+    shape = (rows_at, half)
+    lane = iota(shape, 1)
+    lane_pack = lane >> log_sg
+
+    def taper(pixel):
+        return 1.0 - ((2.0 * pixel.astype(jnp.float32) - (SG - 1)) / SG) ** 2
+
+    tapers = taper(PACK * iota(shape, 0) + lane_pack) * taper(lane & (SG - 1))
+    pixel = iota((SG, 1), 0)
+    y_pixel = pixel.astype(jnp.float32)
+    x_pixel = (PACK * (pixel & (rows_at - 1)) + pixel // rows_at).astype(jnp.float32)
+
+    @pl.loop(0, packs)
+    def _(p):
+        gains = []
+        for n in range(PACK):
+            j = p * PACK + n
+            one_r, one_i = beams[0, 0, j], beams[0, 1, j]
+            two_r, two_i = beams[1, 0, j], beams[1, 1, j]
+            gains.append(
+                ((one_r * two_r + one_i * two_i) * tapers, (one_i * two_r - one_r * two_i) * tapers)
+            )
+            at = slice(n * SG, (n + 1) * SG)
+            real, imag = turn_fraction(uv_ref[1, pl.ds(j, 1)] * y_pixel)
+            for k, (er, ei) in enumerate(zip(split(real), split(imag))):
+                ev[k, p, n * SG:(n + 1) * SG, :half] = er
+                ev[k, p, n * SG:(n + 1) * SG, half:] = ei
+                ev[k, p, half + n * SG:half + (n + 1) * SG, :half] = -ei
+                ev[k, p, half + n * SG:half + (n + 1) * SG, half:] = er
+            uu[0, p, at], uu[1, p, at] = turn_fraction(uv_ref[0, pl.ds(j, 1)] * x_pixel)
+        for part in range(2):
+            for q in range(PACK):
+                picked = None
+                for n in range(PACK):
+                    shift = (n - q) * SG % half
+                    moved = gains[n][part]
+                    moved = pltpu.roll(moved, shift, axis=1) if shift else moved
+                    picked = moved if n == 0 else jnp.where(lane_pack == n, moved, picked)
+                gain[part, p, q * rows_at:(q + 1) * rows_at] = picked
+
+
+def predict_kernel(
     n_stn, n_chan, n_tile,
-    x_ref, off_ref, out_ref,
+    x_ref, off_ref, pair_ref, beam_ref, uv_ref, out_ref,
     full, ar, ai, br, bi, cr, ci, dr, di, tab, eu, cuts, inbox,
-    z_send, y_send, m_send, recv, cut_send, cut_recv,
+    beams, gain, dft_x, dft_y, ev, uu, outbox, box,
+    z_send, y_send, m_send, recv, cut_send, cut_recv, vis_send, vis_recv,
 ):
     stn, chan, tile = lax.axis_index("stn"), lax.axis_index("chan"), lax.axis_index("tile")
     tiles, piece_rows, columns = x_ref.shape
@@ -84,7 +179,7 @@
     sources = [lax.rem(stn + d, n_stn) for d in hops]
 
     barrier = pltpu.get_barrier_semaphore()
-    partners = [{"stn": s} for s in sources] + [{"chan": mate}, {"chan": across}]
+    partners = [{"stn": s} for s in sources] + [{"chan": lax.rem(chan + d, n_chan)} for d in range(1, n_chan)]
     partners += [{"tile": lax.rem(tile + d, n_tile)} for d in range(1, n_tile)]
     for where in partners:
         pl.semaphore_signal(barrier, inc=1, device_id=where, device_id_type=MESH)
@@ -116,9 +211,14 @@
     @pl.loop(0, group // 8)
     def _(step):
         at = pl.multiple_of(step * 8, 8)
-        corners = off_ref[pl.ds(first + at, 8), :]
-        ar[pl.ds(at, 8)], ai[pl.ds(at, 8)] = unit_phase(corners[:, 1:2] * col_pos)
-        cr[pl.ds(at, 8)], ci[pl.ds(at, 8)] = unit_phase(corners[:, 0:1] * row_pos)
+        u_first = jnp.zeros((8, 1), jnp.int32)
+        v_first = u_first
+        for n in range(8):
+            here = iota((8, 1), 0) == n
+            u_first = jnp.where(here, off_ref[0, first + at + n], u_first)
+            v_first = jnp.where(here, off_ref[1, first + at + n], v_first)
+        ar[pl.ds(at, 8)], ai[pl.ds(at, 8)] = unit_phase(v_first * col_pos)
+        cr[pl.ds(at, 8)], ci[pl.ds(at, 8)] = unit_phase(u_first * row_pos)
 
     @pl.loop(0, group // PACK)
     def _(pack):
@@ -143,6 +243,7 @@
             copy = remote(piece, piece, sems.at[slot], recv.at[chan, s], {"chan": where})
             copy.start()
             onward.append(copy)
+    prediction_tables(pair_ref, beam_ref, uv_ref, beams, gain, dft_x, dft_y, ev, uu)
     for n, s in enumerate(sources):
         piece = full.at[across, s]
         remote(piece, piece, y_send.at[n], recv.at[across, s], {"chan": across}).wait_recv()
@@ -166,6 +267,7 @@
 
     packs = SUB_TILE // PACK
     both = 2 * PACK * SG
+    half = PACK * SG
     per_step = 2
     sent = []
     for d in range(1, n_tile + 1):
@@ -202,22 +304,62 @@
     for d, copy in enumerate(sent):
         copy.wait()
         total += inbox[d]
-    out_ref[...] = total
-
-
-def own_cuts_call(model_image, offsets):
+    lines = []
+    for p in range(packs):
+        high, low = split(total[p])
+        z = dot_nn(dft_x[...], jnp.concatenate([high, low, high], axis=0))
+        lines.append(jnp.concatenate([z[:SG], z[SG:]], axis=1))
+    high, low = split(jnp.concatenate(lines, axis=0))
+    sub = dot_nn(high, dft_y[0]) + dot_nn(low, dft_y[0]) + dot_nn(high, dft_y[1])
+    lane_pair = (iota((SG, both), 1) >> (SG.bit_length() - 1)) & (PACK - 1)
+    for p in range(packs):
+        sub_p = sub[p * SG:(p + 1) * SG]
+        real, imag = cmul(sub_p[:, :half], sub_p[:, half:], gain[0, p], gain[1, p])
+        weighted = jnp.concatenate([real, imag], axis=1)
+        apart = [jnp.where(lane_pair == n, weighted, 0.0) for n in range(PACK)]
+        high, low = split(jnp.concatenate(apart, axis=0))
+        inner = dot_nn(high, ev[0, p]) + dot_nn(low, ev[0, p]) + dot_nn(high, ev[1, p])
+        real, imag = cmul(uu[0, p], uu[1, p], inner[:, :half], inner[:, half:])
+        outbox[:, 0, p] = real.reshape(PACK, SG, half).sum(axis=1)
+        outbox[:, 1, p] = imag.reshape(PACK, SG, half).sum(axis=1)
+
+    sent = []
+    for d in range(1, n_chan):
+        to = lax.rem(chan + d, n_chan)
+        copy = remote(
+            outbox.at[to], box.at[chan], vis_send.at[d - 1], vis_recv.at[chan], {"chan": to}
+        )
+        copy.start()
+        sent.append(copy)
+    box[chan] = outbox[chan]
+    for d in range(1, n_chan):
+        source = lax.rem(chan + d, n_chan)
+        remote(
+            outbox.at[source], box.at[source], vis_send.at[d - 1], vis_recv.at[source],
+            {"chan": source},
+        ).wait_recv()
+    for g in range(n_chan):
+        out_ref[:, :, 0, g * half:(g + 1) * half] = box[g]
+    for copy in sent:
+        copy.wait_send()
+
+
+def predict_call(model_image, offsets, pair_ids, station_beams, uv_block):
     n_stn, n_chan, n_tile = (lax.axis_size(a) for a in ("stn", "chan", "tile"))
     tiles, piece_rows, columns = model_image.shape
     rows = n_stn * tiles * piece_rows
     group = SUB_TILE * n_tile
     packs = SUB_TILE // PACK
     f32, bf16 = jnp.float32, jnp.bfloat16
+    half = PACK * SG
+    assert PACK == n_chan
     vmem = pl.BlockSpec(memory_space=pltpu.VMEM)
+    smem = pl.BlockSpec(memory_space=pltpu.SMEM)
     dma = pltpu.SemaphoreType.DMA
     return pl.pallas_call(
-        functools.partial(cuts_kernel, n_stn, n_chan, n_tile),
-        out_shape=jax.ShapeDtypeStruct((packs, 2 * SG, PACK * SG), f32),
-        in_specs=[vmem, vmem],
+        functools.partial(predict_kernel, n_stn, n_chan, n_tile),
+        out_shape=jax.ShapeDtypeStruct((2, packs, 1, n_chan * half), f32),
+        in_specs=[vmem, smem, smem, vmem, vmem],
         out_specs=vmem,
         scratch_shapes=[
             pltpu.VMEM((n_chan, n_stn, tiles, piece_rows, columns // n_chan), bf16),
@@ -233,69 +375,27 @@
             pltpu.VMEM((group * 2 * SG, 2 * rows), bf16),
             pltpu.VMEM((group // PACK, 2 * SG, PACK * SG), f32),
             pltpu.VMEM((max(n_tile - 1, 1), packs, 2 * SG, PACK * SG), f32),
+            pltpu.VMEM((2, 2, SUB_TILE, SG // PACK, half), f32),
+            pltpu.VMEM((2, packs, SG, half), f32),
+            pltpu.VMEM((2 * SG, 6 * SG), bf16),
+            pltpu.VMEM((2, 2 * half, 2 * half), bf16),
+            pltpu.VMEM((2, packs, 2 * half, 2 * half), bf16),
+            pltpu.VMEM((2, packs, half, half), f32),
+            pltpu.VMEM((n_chan, 2, packs, half), f32),
+            pltpu.VMEM((n_chan, 2, packs, half), f32),
             dma((n_stn - 1,)),
             dma((n_stn - 1,)),
             dma((2 * (n_stn - 1),)),
             dma((n_chan, n_stn)),
             dma((max(n_tile - 1, 1),)),
             dma((max(n_tile - 1, 1),)),
+            dma((n_chan - 1,)),
+            dma((n_chan,)),
         ],
         compiler_params=pltpu.CompilerParams(
             collective_id=0, has_side_effects=True, vmem_limit_bytes=60 * 1024 * 1024
         ),
-    )(model_image, offsets)
-
-
-def exact_mix(pattern, left, right):
-    return jnp.einsum(pattern, left, right, precision=lax.Precision.HIGHEST)
-
-
-def predict(cut_rows, pair_ids, station_beams, uv_block):
-    how_many = cut_rows.shape[0]
-    cut_grid = cut_rows.reshape(how_many, 2, SG, SG)
-    pixel_idx = jnp.arange(SG, dtype=jnp.int32)
-    w_real, w_neg = phase_pair(pixel_idx[:, None] * pixel_idx[None, :], SG)
-    w_imag = -w_neg
-    c_real = cut_grid[:, 0]
-    c_imag = cut_grid[:, 1]
-    half_real = exact_mix("xa,jab->jxb", w_real, c_real) - exact_mix("xa,jab->jxb", w_imag, c_imag)
-    half_imag = exact_mix("xa,jab->jxb", w_real, c_imag) + exact_mix("xa,jab->jxb", w_imag, c_real)
-    sub_real = (
-        exact_mix("jxb,yb->jxy", half_real, w_real) - exact_mix("jxb,yb->jxy", half_imag, w_imag)
-    ) / (SG * SG)
-    sub_imag = (
-        exact_mix("jxb,yb->jxy", half_real, w_imag) + exact_mix("jxb,yb->jxy", half_imag, w_real)
-    ) / (SG * SG)
-    pixel_pos = pixel_idx.astype(jnp.float32)
-    taper_line = 1.0 - ((2.0 * pixel_pos - (SG - 1)) / SG) ** 2
-    taper_grid = (taper_line[:, None] * taper_line[None, :]).reshape(SG * SG)
-    beam_first = station_beams[:, pair_ids[:, 0]]
-    beam_second = station_beams[:, pair_ids[:, 1]]
-    gain_real = (beam_first[0] * beam_second[0] + beam_first[1] * beam_second[1]) * taper_grid
-    gain_imag = (beam_first[1] * beam_second[0] - beam_first[0] * beam_second[1]) * taper_grid
-    flat_real = sub_real.reshape(how_many, SG * SG)
-    flat_imag = sub_imag.reshape(how_many, SG * SG)
-    weighted_real = (flat_real * gain_real - flat_imag * gain_imag).reshape(how_many, SG, SG)
-    weighted_imag = (flat_real * gain_imag + flat_imag * gain_real).reshape(how_many, SG, SG)
-    u_angle = uv_block[0][:, :, None] * pixel_pos[None, None, :] * (two_pi / SG)
-    v_angle = uv_block[1][:, :, None] * pixel_pos[None, None, :] * (two_pi / SG)
-    eu_real = jnp.cos(u_angle)
-    eu_imag = -jnp.sin(u_angle)
-    ev_real = jnp.cos(v_angle)
-    ev_imag = -jnp.sin(v_angle)
-    inner_real = exact_mix("jxy,jky->jxk", weighted_real, ev_real) - exact_mix(
-        "jxy,jky->jxk", weighted_imag, ev_imag
-    )
-    inner_imag = exact_mix("jxy,jky->jxk", weighted_real, ev_imag) + exact_mix(
-        "jxy,jky->jxk", weighted_imag, ev_real
-    )
-    vis_real = exact_mix("jkx,jxk->jk", eu_real, inner_real) - exact_mix(
-        "jkx,jxk->jk", eu_imag, inner_imag
-    )
-    vis_imag = exact_mix("jkx,jxk->jk", eu_real, inner_imag) + exact_mix(
-        "jkx,jxk->jk", eu_imag, inner_real
-    )
-    return jnp.stack([vis_real, vis_imag], axis=0)
+    )(model_image, offsets.T, pair_ids.T, station_beams, uv_block)
 
 
 def on_device(
@@ -307,13 +407,9 @@
     observed,
     live_counts,
 ):
-    packed = own_cuts_call(model_image, subgrid_offsets[0])
-    own_cuts = packed.reshape(SUB_TILE // PACK, 2, SG, PACK, SG).transpose(0, 3, 1, 2, 4)
-    own_cuts = own_cuts.reshape(SUB_TILE, 2 * SG * SG)
-    predicted = predict(own_cuts, subgrid_stations, station_beams, visibility_uv)
-    chan_count = lax.axis_size("chan")
-    outgoing = predicted.reshape(2, SUB_TILE // chan_count, chan_count, predicted.shape[2])
-    regrouped = lax.all_to_all(outgoing, "chan", split_axis=2, concat_axis=3, tiled=True)
+    regrouped = predict_call(
+        model_image, subgrid_offsets[0], subgrid_stations, station_beams, visibility_uv
+    )
     total_rows = regrouped.shape[3]
     time_step = jnp.mod(jnp.arange(total_rows, dtype=jnp.int32), TIMES)
     live_mask = time_step[None, None, :] < live_counts[:, :, None]

time: 52.9 us -> 32.5 us (0.61)
  matrix products: 10.4 us -> 0 us
  local copies, waits for them, and re-layouts: 8.02 us -> 0.65 us
  starting transfers between devices: 3.25 us -> 0 us
  waiting for transfers between devices: 3.08 us -> 0 us
  Pallas kernels: 27.3 us -> 30.1 us
  other arithmetic: 0.22 us -> 1.43 us
    dot_general x12 -> x0, matrix products: 10.4 us -> none  [exact_mix(): return jnp.einsum(pattern, left, right, precision=lax.Precision.HIGHEST)]
    all_to_all x1 -> x0, starting transfers between devices: 3.25 us -> none  [on_device(): lax.all_to_all(outgoing, 'chan', split_axis=2, concat_axis=3, tiled=True)]
    all_to_all x1 -> x0, waiting for transfers between devices: 3.08 us -> none  [on_device(): lax.all_to_all(outgoing, 'chan', split_axis=2, concat_axis=3, tiled=True)]
    unnamed x11 -> x4, local copies, waits for them, and re-layouts: 3.69 us -> 0.65 us
    pallas_call x1, Pallas kernels: 27.3 us -> 30.1 us  [predict_call(): pl.pallas_call(functools.partial(predict_kernel, n_stn, n_chan, n_tile),...]
    gather x2 -> x0, local copies, waits for them, and re-layouts: 1.48 us -> none  [the longest x1 0.74 us: predict(): beam_first = station_beams[:, pair_ids[:, 0]]]
    select_n x1, other arithmetic: 0.01 us -> 1.35 us  [on_device(): return jnp.where(live_mask[None], observed - regrouped, 0.0)]
    reshape x1 -> x0, local copies, waits for them, and re-layouts: 1.16 us -> none  [on_device(): packed.reshape(SUB_TILE // PACK, 2, SG, PACK, SG).transpose(0, 3, 1, 2, 4)]
  transfers between devices with their start and end apart: 1 -> 0, of which waited for: 1 -> 0; matrix products, arithmetic and copies ran while one was open for 0% -> 0% of each run, Pallas kernels for 0% -> 0%
where the time goes in v2:
time: 32.5 us; the launch traced here: 32.2 us
  Pallas kernels  30.1 us (93%)
  other arithmetic  1.43 us (4%)
  local copies, waits for them, and re-layouts  0.65 us (2%)
    pallas_call x1, Pallas kernels, predict_call(): pl.pallas_call(functools.partial(predict_kernel, n_stn, n_chan, n_tile),...  30.1 us
    select_n x1, other arithmetic, on_device(): return jnp.where(live_mask[None], observed - regrouped, 0.0)  1.35 us
    unnamed x4, local copies, waits for them, and re-layouts  0.65 us

profile of v2, /device:TPU:0, one launch (start us, length us, event | category | flops | bytes accessed | tf_op | source)
XLA Modules:
  0.0 32.2 jit_solution(296701022267552516)
XLA Ops:
  0.0 0.0 copy-start.1
  0.0 0.6 %copy-done.1 = s32[4,1]{0,1:T(1,128)S(1)} copy-done((s32[4,1]{0,1:T(1,128)S(1)}, s32[4,1]{0,1:T(1,128)}, u32[]{:S(2)}) %copy-start.1) | copy-done | bytes 40
  0.7 0.1 broadcast_compare_fusion
  0.7 0.0 copy-start
  0.7 30.1 %shard_map.73 = f32[2,4,1,512]{3,2,1,0:T(1,128)} custom-call(bf16[4,16,2048]{2,1,0:T(8,128)(2,1)} %x_ref.1, s32[2,128]{1,0:T(2,128)} %bitcast.5, s32[2,16]{1,0:T(2,128)} %bitcast.6, f32[2,64,1024]{2,1,0:T(8,128)} %beam_ref.1, f32[2,16,128]{2,1,0:T(8,128)} %uv_ref.1), custom_call_target="tpu_custom_call" | custom-call | tf_op jit(solution)/shard_map/pallas_call | solution.py:359
  30.9 0.0 copy-done
  30.9 1.3 %broadcast_select_fusion = f32[2,4,1,512]{3,2,1,0:T(1,128)} fusion(pred[4,512]{1,0:T(4,128)(4,1)S(1)} %broadcast_compare_fusion, f32[2,4,1,512]{3,2,1,0:T(1,128)S(1)} %copy-done, f32[2,4,1,512]{3,2,1,0:T(1,128)} %shard_map.73), kind=kLoop, calls=%fused_computation | loop fusion | flops 8192 | bytes 51200 | tf_op jit(solution)/shard_map/jit(_where)/select_n | solution.py:416
  (1 shorter events, 0.0 us)
Async XLA Ops:
  0.0 0.7 %copy-start.1 = (s32[4,1]{0,1:T(1,128)S(1)}, s32[4,1]{0,1:T(1,128)}, u32[]{:S(2)}) copy-start(s32[4,1]{0,1:T(1,128)} %param.13) | copy-start | bytes 52
  0.7 30.1 %copy-start = (f32[2,4,1,512]{3,2,1,0:T(1,128)S(1)}, f32[2,4,1,512]{3,2,1,0:T(1,128)}, u32[]{:S(2)}) copy-start(f32[2,4,1,512]{3,2,1,0:T(1,128)} %param.12) | copy-start | bytes 49156

commit v3 on v2

--- a/solution.py
+++ b/solution.py
@@ -13,6 +13,7 @@
 TILE_DEV = 4
 TL = 64
 SUB_TILE = 16
+CUTS = 1
 PACK = 4
 
 MESH = pl.DeviceIdType.MESH
@@ -163,10 +164,10 @@
 
 def predict_kernel(
     n_stn, n_chan, n_tile,
-    x_ref, off_ref, pair_ref, beam_ref, uv_ref, out_ref,
+    x_ref, off_ref, pair_ref, live_ref, beam_hbm, uv_ref, seen_ref, out_ref,
     full, ar, ai, br, bi, cr, ci, dr, di, tab, eu, cuts, inbox,
-    beams, gain, dft_x, dft_y, ev, uu, outbox, box,
-    z_send, y_send, m_send, recv, cut_send, cut_recv, vis_send, vis_recv,
+    beam_ref, beams, gain, dft_x, dft_y, ev, uu, outbox, box,
+    z_send, y_send, m_send, recv, cut_send, cut_recv, vis_send, vis_recv, beam_sem,
 ):
     stn, chan, tile = lax.axis_index("stn"), lax.axis_index("chan"), lax.axis_index("tile")
     tiles, piece_rows, columns = x_ref.shape
@@ -178,6 +179,8 @@
     hops = [1, n_stn - 1] + list(range(2, n_stn - 1))
     sources = [lax.rem(stn + d, n_stn) for d in hops]
 
+    beam_copy = pltpu.make_async_copy(beam_hbm, beam_ref, beam_sem)
+    beam_copy.start()
     barrier = pltpu.get_barrier_semaphore()
     partners = [{"stn": s} for s in sources] + [{"chan": lax.rem(chan + d, n_chan)} for d in range(1, n_chan)]
     partners += [{"tile": lax.rem(tile + d, n_tile)} for d in range(1, n_tile)]
@@ -185,10 +188,20 @@
         pl.semaphore_signal(barrier, inc=1, device_id=where, device_id_type=MESH)
     pl.semaphore_wait(barrier, len(partners))
 
-    own = x_ref.at[:, :, pl.ds(pl.multiple_of(chan * quarter, quarter), quarter)]
+    share = tiles // CUTS
+    travels = [(s, h) for s in sources for h in range(CUTS)]
+
+    def own(h):
+        return x_ref.at[
+            pl.ds(h * share, share), :, pl.ds(pl.multiple_of(chan * quarter, quarter), quarter)
+        ]
+
+    def piece(c, s, h):
+        return full.at[c, s, pl.ds(h * share, share)]
+
     z_copies = [
-        remote(own, full.at[chan, stn], z_send.at[n], recv.at[chan, stn], {"stn": s})
-        for n, s in enumerate(sources)
+        remote(own(h), piece(chan, stn, h), z_send.at[n], recv.at[chan, stn, h], {"stn": s})
+        for n, (s, h) in enumerate(travels)
     ]
     for copy in z_copies:
         copy.start()
@@ -236,24 +249,34 @@
             eu[pl.ds(base + (PACK + n) * SG, SG), rows:] = real
 
     onward = []
-    for n, s in enumerate(sources):
-        piece = full.at[chan, s]
-        remote(own, piece, z_send.at[n], recv.at[chan, s], {"stn": s}).wait_recv()
-        for sems, slot, where in ((y_send, n, across), (m_send, n, mate)):
-            copy = remote(piece, piece, sems.at[slot], recv.at[chan, s], {"chan": where})
-            copy.start()
-            onward.append(copy)
-    prediction_tables(pair_ref, beam_ref, uv_ref, beams, gain, dft_x, dft_y, ev, uu)
-    for n, s in enumerate(sources):
-        piece = full.at[across, s]
-        remote(piece, piece, y_send.at[n], recv.at[across, s], {"chan": across}).wait_recv()
-        copy = remote(piece, piece, m_send.at[len(sources) + n], recv.at[across, s], {"chan": mate})
+
+    def forward(c, n, sems, slot, to):
+        s, h = travels[n]
+        copy = remote(
+            piece(c, s, h), piece(c, s, h), sems.at[slot], recv.at[c, s, h], {"chan": to}
+        )
         copy.start()
         onward.append(copy)
-    for n, s in enumerate(sources):
-        for c in (mate, mate ^ 2):
-            piece = full.at[c, s]
-            remote(piece, piece, y_send.at[n], recv.at[c, s], {"chan": mate}).wait_recv()
+
+    def arrive(c, n, source):
+        s, h = travels[n]
+        remote(piece(c, s, h), piece(c, s, h), z_send.at[n], recv.at[c, s, h], source).wait_recv()
+
+    def pass_across(n):
+        arrive(across, n, {"chan": across})
+        forward(across, n, m_send, len(travels) + n, mate)
+
+    for n, (s, h) in enumerate(travels):
+        arrive(chan, n, {"stn": s})
+        forward(chan, n, y_send, n, across)
+        forward(chan, n, m_send, n, mate)
+    beam_copy.wait()
+    prediction_tables(pair_ref, beam_ref, uv_ref, beams, gain, dft_x, dft_y, ev, uu)
+    for n in range(len(travels)):
+        pass_across(n)
+    for n in range(len(travels)):
+        arrive(mate, n, {"chan": mate})
+        arrive(mate ^ 2, n, {"chan": mate})
     for copy in z_copies + onward:
         copy.wait_send()
 
@@ -339,12 +362,18 @@
             {"chan": source},
         ).wait_recv()
     for g in range(n_chan):
-        out_ref[:, :, 0, g * half:(g + 1) * half] = box[g]
+        at = slice(g * half, (g + 1) * half)
+        time_step = lax.rem(iota((1, half), 1) + g * half, TIMES)
+        for p in range(packs):
+            live = time_step < live_ref[0, p]
+            for k in range(2):
+                seen = seen_ref[k, p, :, at]
+                out_ref[k, p, :, at] = jnp.where(live, seen - box[g, k, p:p + 1], 0.0)
     for copy in sent:
         copy.wait_send()
 
 
-def predict_call(model_image, offsets, pair_ids, station_beams, uv_block):
+def predict_call(model_image, offsets, pair_ids, live, station_beams, uv_block, observed):
     n_stn, n_chan, n_tile = (lax.axis_size(a) for a in ("stn", "chan", "tile"))
     tiles, piece_rows, columns = model_image.shape
     rows = n_stn * tiles * piece_rows
@@ -358,8 +387,8 @@
     dma = pltpu.SemaphoreType.DMA
     return pl.pallas_call(
         functools.partial(predict_kernel, n_stn, n_chan, n_tile),
-        out_shape=jax.ShapeDtypeStruct((2, packs, 1, n_chan * half), f32),
-        in_specs=[vmem, smem, smem, vmem, vmem],
+        out_shape=jax.ShapeDtypeStruct(observed.shape, f32),
+        in_specs=[vmem, smem, smem, smem, pl.BlockSpec(memory_space=pl.ANY), vmem, vmem],
         out_specs=vmem,
         scratch_shapes=[
             pltpu.VMEM((n_chan, n_stn, tiles, piece_rows, columns // n_chan), bf16),
@@ -375,6 +404,7 @@
             pltpu.VMEM((group * 2 * SG, 2 * rows), bf16),
             pltpu.VMEM((group // PACK, 2 * SG, PACK * SG), f32),
             pltpu.VMEM((max(n_tile - 1, 1), packs, 2 * SG, PACK * SG), f32),
+            pltpu.VMEM(station_beams.shape, f32),
             pltpu.VMEM((2, 2, SUB_TILE, SG // PACK, half), f32),
             pltpu.VMEM((2, packs, SG, half), f32),
             pltpu.VMEM((2 * SG, 6 * SG), bf16),
@@ -383,19 +413,20 @@
             pltpu.VMEM((2, packs, half, half), f32),
             pltpu.VMEM((n_chan, 2, packs, half), f32),
             pltpu.VMEM((n_chan, 2, packs, half), f32),
-            dma((n_stn - 1,)),
-            dma((n_stn - 1,)),
-            dma((2 * (n_stn - 1),)),
-            dma((n_chan, n_stn)),
+            dma((CUTS * (n_stn - 1),)),
+            dma((CUTS * (n_stn - 1),)),
+            dma((2 * CUTS * (n_stn - 1),)),
+            dma((n_chan, n_stn, CUTS)),
             dma((max(n_tile - 1, 1),)),
             dma((max(n_tile - 1, 1),)),
             dma((n_chan - 1,)),
             dma((n_chan,)),
+            pltpu.SemaphoreType.DMA,
         ],
         compiler_params=pltpu.CompilerParams(
             collective_id=0, has_side_effects=True, vmem_limit_bytes=60 * 1024 * 1024
         ),
-    )(model_image, offsets.T, pair_ids.T, station_beams, uv_block)
+    )(model_image, offsets.T, pair_ids.T, live.T, station_beams, uv_block, observed)
 
 
 def on_device(
@@ -407,13 +438,10 @@
     observed,
     live_counts,
 ):
-    regrouped = predict_call(
-        model_image, subgrid_offsets[0], subgrid_stations, station_beams, visibility_uv
-    )
-    total_rows = regrouped.shape[3]
-    time_step = jnp.mod(jnp.arange(total_rows, dtype=jnp.int32), TIMES)
-    live_mask = time_step[None, None, :] < live_counts[:, :, None]
-    return jnp.where(live_mask[None], observed - regrouped, 0.0)
+    return predict_call(
+        model_image, subgrid_offsets[0], subgrid_stations, live_counts, station_beams,
+        visibility_uv, observed,
+    )
 
 
 def solution(mesh):

time: 32.5 us -> 31.6 us (0.972)
  other arithmetic: 1.43 us -> 0 us
  local copies, waits for them, and re-layouts: 0.65 us -> 1.32 us
    select_n x2 -> x0, other arithmetic: 1.35 us -> none  [the longest x1 1.35 us: on_device(): return jnp.where(live_mask[None], observed - regrouped, 0.0)]
    unnamed x4 -> x1, local copies, waits for them, and re-layouts: 0.65 us -> 1.32 us
where the time goes in v3:
time: 31.6 us; the launch traced here: 31.3 us
  Pallas kernels  30 us (95%)
  local copies, waits for them, and re-layouts  1.32 us (4%)
    pallas_call x1, Pallas kernels, predict_call(): pl.pallas_call(functools.partial(predict_kernel, n_stn, n_chan, n_tile),...  30 us
    unnamed x1, local copies, waits for them, and re-layouts  1.32 us

profile of v3, /device:TPU:0, one launch (start us, length us, event | category | flops | bytes accessed | tf_op | source)
XLA Modules:
  0.0 31.3 jit_solution(8000369894885952632)
XLA Ops:
  0.0 30.0 %shard_map.73 = f32[2,4,1,512]{3,2,1,0:T(1,128)} custom-call(bf16[4,16,2048]{2,1,0:T(8,128)(2,1)} %x_ref.1, s32[2,128]{1,0:T(2,128)} %bitcast.5, s32[2,16]{1,0:T(2,128)} %bitcast.6, s32[1,4]{1,0:T(1,128)} %bitcast.7, f32[2,64,1024]{2,1,0:T(8,128)} %beam_hbm.1, f32[2,16,128]{2,1,0:T(8,128)} %uv_ref.1, f32[2,4,1,512]{3,2,1,0:T(1,128)} %seen_ref.1), custom_call_target="tpu_custom_call" | custom-call | tf_op jit(solution)/shard_map/pallas_call | solution.py:388
  30.0 1.3 %copy.9 = f32[2,4,1,512]{3,2,1,0:T(1,128)} copy(f32[2,4,1,512]{3,2,1,0:T(1,128)} %shard_map.73) | data formatting | bytes 32768
